TPU v7x, 32 devices: a whole 2x2x4 slice. The times are simulated.
32 devices in a mesh: lat: 2 (over x), lon: 2 (over y), lev: 8 (over z, core).
Axes of the slice: x: 2, y: 2, z: 4, core: 2. Of those that a mesh axis runs over, the one named last changes fastest.
Arguments:
- along_axis_flow: bfloat16 [80, 4, 32, 1440], P(('lat', 'lev'), None, None, 'lon'), may hold values from -6 to 6
- poleward_flow: bfloat16 [80, 4, 32, 1440], P(('lat', 'lev'), None, None, 'lon'), may hold values from -6 to 6
- warmth_departure: bfloat16 [80, 4, 32, 1440], P(('lat', 'lev'), None, None, 'lon'), may hold values from -6 to 6
- validity_indicator: int32 [80, 32, 1440], P(('lat', 'lev'), None, 'lon'), may hold values from 0 to 1
- layer_depth_span: float32 [32], replicated, may hold values from 0.3 to 3
- desired_circulation_norm: float32 [80, 4, 32], P(('lat', 'lev')), may hold values from -4 to 4
Outputs:
- psi_norm: float32 [80, 4, 32], P(('lat', 'lev'))
- heat_cospec: float32 [720, 80, 128], P('lon', ('lat', 'lev'))
- momentum_cospec: float32 [720, 80, 128], P('lon', ('lat', 'lev'))
- budget_penalty: float32 [], replicated
All inputs are finite; a program needn't handle non-finite values. Where the computation divides by a largest or mean magnitude, that divisor is 1e-20 or more.
Results may differ from a plain program's by a relative error of at most 0.0033.
Values may be sent and summed in bfloat16 or wider, within the bound.
A program may use at most 64 MiB of HBM per device.

v0:
```python
import math

import jax
import jax.numpy as jnp
from jax import lax
from jax.sharding import PartitionSpec as P

GRID_MERIDIANS = 1440
HARMONIC_ORDERS = 720


epsilon = 1e-06


def entering(value, axis, join, neutral):
    count, mine = (lax.axis_size(axis), lax.axis_index(axis))
    pieces = lax.all_gather(value, axis)
    so_far = jnp.full_like(value, 0) + jnp.asarray(neutral, value.dtype)

    def step(position, so_far):
        longer = join(so_far, pieces[position])
        return jnp.where(position < mine, longer, so_far)

    return lax.fori_loop(0, count - 1, step, so_far)


def build_waves(wave_rows, lon_index):
    wavenumber = wave_rows // 2 + 1
    component = wave_rows % 2
    turns = wavenumber[:, None] * lon_index[None, :] % GRID_MERIDIANS
    angle = turns.astype(jnp.float32) * (2.0 * math.pi / GRID_MERIDIANS)
    return jnp.where(component[:, None] == 0, jnp.cos(angle), jnp.sin(angle)).astype(jnp.bfloat16)


def add_arrays(earlier, later):
    return earlier + later


def cospectra(fourier_weights, norm_factor):
    heat_part = norm_factor * (
        fourier_weights[:, 0, 1] * fourier_weights[:, 0, 2]
        + fourier_weights[:, 1, 1] * fourier_weights[:, 1, 2]
    )
    moment_part = norm_factor * (
        fourier_weights[:, 0, 0] * fourier_weights[:, 0, 1]
        + fourier_weights[:, 1, 0] * fourier_weights[:, 1, 1]
    )
    return (heat_part, moment_part)


def per_device(
    along_axis_flow,
    poleward_flow,
    warmth_departure,
    validity_indicator,
    layer_depth_span,
    desired_circulation_norm,
):
    bands, batch, level_values, lon_count = poleward_flow.shape
    lon_ways = lax.axis_size("lon")
    retained_indicator = validity_indicator.astype(jnp.bfloat16)[:, None]
    screened_eastward_speed = along_axis_flow * retained_indicator
    screened_northward_speed = poleward_flow * retained_indicator
    screened_thermal_anomaly = warmth_departure * retained_indicator
    zonal_v = jnp.sum(screened_northward_speed, axis=3, dtype=jnp.float32)
    kept_count = jnp.sum(validity_indicator, axis=2).astype(jnp.float32)
    zonal_v, kept_count = lax.psum((zonal_v, kept_count), "lon")
    mean_v = zonal_v / jnp.maximum(kept_count, 1.0)[:, None, :]
    columns = batch * level_values
    joined_arrays = jnp.stack(
        [screened_eastward_speed, screened_northward_speed, screened_thermal_anomaly]
    ).reshape(3, bands, columns, lon_count)
    norm_factor = 2.0 / (GRID_MERIDIANS * GRID_MERIDIANS)
    wave_local = HARMONIC_ORDERS // lon_ways
    own_rows = lax.axis_index("lon") * (2 * wave_local) + jnp.arange(
        2 * wave_local, dtype=jnp.int32
    )
    waves_table = build_waves(own_rows, jnp.arange(GRID_MERIDIANS, dtype=jnp.int32))
    fourier_weights = lax.dot_general(
        waves_table,
        lax.all_gather(joined_arrays, "lon", axis=3, tiled=True),
        (((1,), (3,)), ((), ())),
        preferred_element_type=jnp.float32,
    )
    fourier_weights = fourier_weights.reshape(wave_local, 2, 3, bands, columns)
    heat_cospec, momentum_cospec = cospectra(fourier_weights, norm_factor)
    nlat = bands * lax.axis_size(("lat", "lev"))
    band_index = lax.axis_index(("lat", "lev")) * bands + jnp.arange(bands, dtype=jnp.int32)
    latitude = ((band_index.astype(jnp.float32) + 0.5) / nlat - 0.5) * math.pi
    cosine = jnp.cos(latitude)
    weighted = mean_v * cosine[:, None, None] * layer_depth_span[None, None, :]
    upward = jnp.cumsum(weighted, axis=2)
    southward = jnp.cumsum(upward, axis=0)
    band_sums = southward[-1]
    southern = entering(
        band_sums, ("lat", "lev"), add_arrays, jnp.zeros((batch, level_values), jnp.float32)
    )
    stream = southward + southern[None]
    local_peak = jnp.max(jnp.abs(stream))
    cell_count = batch * level_values * nlat
    weight_lat = cosine[:, None, None]
    peak_value = lax.pmax(local_peak, ("lat", "lev"))
    psi_norm = stream / (peak_value + epsilon)
    local_misfit = jnp.sum(weight_lat * (psi_norm - desired_circulation_norm) ** 2)
    budget_penalty = lax.psum(local_misfit, ("lat", "lev")) / cell_count
    return (psi_norm, heat_cospec, momentum_cospec, budget_penalty)


def solution(mesh):
    placed = (
        P(("lat", "lev"), None, None, "lon"),
        P(("lat", "lev"), None, None, "lon"),
        P(("lat", "lev"), None, None, "lon"),
        P(("lat", "lev"), None, "lon"),
        P(),
        P(("lat", "lev"), None, None),
    )
    return jax.shard_map(
        per_device,
        mesh=mesh,
        in_specs=placed,
        out_specs=(
            P(("lat", "lev"), None, None),
            P("lon", ("lat", "lev"), None),
            P("lon", ("lat", "lev"), None),
            P(),
        ),
        check_vma=False,
    )
```

profile of v0, /device:TPU:0, one launch (start us, length us, event | category | flops | bytes accessed | tf_op | source)
XLA Modules:
  0.0 153.3 jit_solution(9562012190459497861)
XLA Ops:
  7.2 0.0 all-gather.2.cloned.1.call-start
  7.2 1.4 fusion.24
  8.6 1.5 %convert_reduce_fusion = (f32[5,4,32]{2,1,0:T(4,128)S(1)}, bf16[5,4,32,720]{3,2,1,0:T(8,128)(2,1)S(1)}) fusion(bf16[5,4,32,720]{3,2,1,0:T(8,128)(2,1)} %param.9, bf16[5,32,720]{2,1,0:T(8,128)(2,1)S(1)} %get-tuple-element.122), kind=kLoop, calls=%fused_computation.17 | loop fusion | flops 1381760 | bytes 2076160 | tf_op jit(solution)/shard_map/reduce_sum | solution.py:65
  10.1 0.8 copy.29
  11.0 1.7 %broadcast_multiply_fusion.1 = (bf16[5,4,32,720]{3,2,1,0:T(8,128)(2,1)S(1)}, bf16[5,4,32,720]{3,2,1,0:T(8,128)(2,1)S(1)}) fusion(bf16[5,4,32,720]{3,2,1,0:T(8,128)(2,1)} %param.8, bf16[5,32,720]{2,1,0:T(8,128)(2,1)S(1)} %get-tuple-element.122, bf16[5,4,32,720]{3,2,1,0:T(8,128)(2,1)} %param.10), kind=kLoop, calls=%fused_computation.21 | loop fusion | flops 921600 | bytes 3916800 | tf_op jit(solution)/shard_map/mul | solution.py:62
  12.6 1.3 copy.28
  13.9 0.8 copy.30
  14.7 0.0 copy-start.1
  14.8 0.0 copy-start
  14.8 3.0 %pad_maximum_fusion = bf16[3,5,128,720]{2,3,1,0:T(8,128)(2,1)} fusion(bf16[1,5,128,720]{2,3,1,0:T(8,128)(2,1)S(1)} %copy.30, bf16[1,5,128,720]{2,3,1,0:T(8,128)(2,1)S(1)} %copy.29, bf16[1,5,128,720]{2,3,1,0:T(8,128)(2,1)} %copy.28), kind=kLoop, calls=%fused_computation.9 | loop fusion | flops 2764800 | bytes 5529600 | tf_op jit(solution)/shard_map/stack | solution.py:70
  17.8 0.0 all-gather.2.cloned.1.call-update
  17.9 9.6 %all-reduce = (f32[5,4,32]{2,1,0:T(4,128)S(1)}, f32[5,32]{1,0:T(8,128)S(1)}) all-reduce(f32[5,4,32]{2,1,0:T(4,128)S(1)} %get-tuple-element.111, f32[5,32]{1,0:T(8,128)S(1)} %convert_element_type.24), channel_id=1, replica_groups=mesh['lat'=2,'lon'=2,'lev'=8] {'lon'}, use_global_device_ids=true, to_apply=%region_1.0 | all-reduce | flops 800 | bytes 6400 | tf_op jit(solution)/shard_map/psum | solution.py:67
  27.6 0.1 multiply_multiply_fusion
  27.6 1.0 reduce_window_sum.22
  28.7 21.7 %all_gather.6 = f32[16,4,32]{2,1,0:T(4,128)S(1)} all-gather(f32[1,4,32]{2,1,0:T(4,128)S(1)} %slice.30), channel_id=1, replica_groups=mesh['lat'=2,'lon'=2,'lev'=8] {'lat','lev'}, dimensions={0}, use_global_device_ids=true | all-gather | bytes 8704 | tf_op jit(solution)/shard_map/all_gather | solution.py:17
  50.3 0.5 while.14
  50.9 0.6 abs_reduce_fusion
  51.5 30.4 %pmax.7 = f32[]{:T(128)} all-reduce(f32[]{:T(128)} %abs_reduce_fusion), channel_id=1, replica_groups=mesh['lat'=2,'lon'=2,'lev'=8] {'lat','lev'}, use_global_device_ids=true, to_apply=%region_9.10 | all-reduce | flops 1 | bytes 8 | tf_op jit(solution)/shard_map/pmax | solution.py:102
  82.6 1.2 multiply_reduce_fusion
  83.8 30.1 %psum.23 = f32[]{:T(128)} all-reduce(f32[]{:T(128)} %get-tuple-element.109), channel_id=1, replica_groups=mesh['lat'=2,'lon'=2,'lev'=8] {'lat','lev'}, use_global_device_ids=true, to_apply=%region_11.12 | all-reduce | flops 1 | bytes 8 | tf_op jit(solution)/shard_map/psum | solution.py:105
  114.6 0.0 all-gather.2.cloned.1.call-done
  114.6 25.1 %fusion.6 = f32[720,3,5,128]{3,0,2,1:T(8,128)S(1)} fusion(bf16[3,5,128,1440]{2,3,1,0:T(8,128)(2,1)} %all-gather.2.cloned.1.call-done, s32[720]{0:T(1024)S(1)} %fusion.14, pred[720]{0:T(1024)(128)(4,1)S(1)} %fusion.13), kind=kOutput, calls=%fused_computation.11 | convolution fusion | flops 3992716800 | bytes 11062800 | tf_op jit(solution)/shard_map/dot_general | solution.py:79
  139.7 3.9 %fusion.23 = (f32[360,1,1,5,128]{4,1,0,3,2:T(1,128)S(1)}, f32[360,1,1,5,128]{4,1,0,3,2:T(1,128)S(1)}, f32[360,1,1,5,128]{4,1,0,3,2:T(1,128)S(1)}, f32[360,1,1,5,...) fusion(f32[360,2,3,5,128]{4,1,0,3,2:T(2,128)S(1)} %bitcast.28), kind=kLoop, calls=%fused_computation.46 | loop fusion | bytes 11059200 | tf_op jit(solution)/shard_map/slice | solution.py:45
  143.6 1.7 %multiply_bitcast_fusion = (f32[360,5,128]{2,0,1:T(8,128)}, f32[360,5,128]{2,0,1:T(8,128)}) fusion(f32[360,1,1,5,128]{4,0,3,2,1:T(8,128)S(1)} %bitcast.37, f32[360,1,1,5,128]{4,0,3,2,1:T(8,128)S(1)} %bitcast.34, f32[360,1,1,5,128]{4,0,3,2,1:T(8,128)S(1)} %bitcast.32, f32[360,1,1,5,128]{4,0,3,2,1:T(8,128)S(1)} %bitcast.36, ...), kind=kLoop, calls=%fused_computation.18 | loop fusion | flops 1843200 | bytes 7372800 | tf_op jit(solution)/shard_map/mul | solution.py:44
  (25 shorter events, 0.3 us)
Async XLA Ops:
  7.2 107.4 %all-gather.2.cloned.1.call-start = ((), (), s32[]{:S(2)}) async-start(), calls=%async_computation | async-start | bytes 8294400 | tf_op jit(solution)/shard_map/all_gather | solution.py:81
  14.7 12.8 %copy-start.1 = (f32[32]{0:T(128)S(1)}, f32[32]{0:T(128)}, u32[]{:S(2)}) copy-start(f32[32]{0:T(128)} %param.12) | copy-start | bytes 388
  14.8 67.8 %copy-start = (f32[5,4,32]{2,1,0:T(4,128)S(1)}, f32[5,4,32]{2,1,0:T(4,128)}, u32[]{:S(2)}) copy-start(f32[5,4,32]{2,1,0:T(4,128)} %param.13) | copy-start | bytes 7684
Sparse Core Ops, SparseCore 0:
  17.9 74.4 all-gather.1
where the time goes:
time: 154 us; the launch traced here: 153 us
  blocking collectives  91.9 us (60%)
  matrix products  25.1 us (16%)
  between operations  16.6 us (11%)
  other arithmetic  12.6 us (8%)
  local copies, waits for them, and re-layouts  6.79 us (4%)
    pmax x1, blocking collectives, per_device(): peak_value = lax.pmax(local_peak, ('lat', 'lev'))  30.4 us
    psum x1, blocking collectives, per_device(): budget_penalty = lax.psum(local_misfit, ('lat', 'lev')) / cell_count  30.1 us
    dot_general x1, matrix products, per_device(): lax.dot_general(waves_table, lax.all_gather(joined_arrays, 'lon', axis=3,...  25.1 us
    all_gather x1, blocking collectives, entering(): pieces = lax.all_gather(value, axis)  21.7 us
    psum x1, blocking collectives, per_device(): zonal_v, kept_count = lax.psum((zonal_v, kept_count), 'lon')  9.64 us
    slice x1, local copies, waits for them, and re-layouts, cospectra(): fourier_weights[:, 0, 0] * fourier_weights[:, 0, 1]  3.85 us
  transfers between devices with their start and end apart: 1, of which 0 were waited for; matrix products, arithmetic and copies ran while one was open for 2% of the time, Pallas kernels for 0%

commit v1 on v0

v1 whole, which is shorter than its diff:
```python
import functools
import math

import jax
import jax.numpy as jnp
import numpy as np
from jax import lax
from jax.experimental import pallas as pl
from jax.experimental.pallas import tpu as pltpu
from jax.sharding import PartitionSpec as P

HARMONIC_ORDERS = 720
epsilon = 1e-06
F32 = jnp.float32
BF16 = jnp.bfloat16


def round_up(value, step):
    return -(-value // step) * step


def wave_table(meridians, parts, rows, padded, span):
    wavenumber = np.arange(1, HARMONIC_ORDERS + 1, dtype=np.int64)
    turns = (wavenumber[:, None] * np.arange(span)[None, :]) % meridians
    angle = turns.astype(np.float32) * np.float32(2.0 * math.pi / meridians)
    waves = np.stack([np.cos(angle), np.sin(angle)]).astype(np.float32)
    waves = waves.reshape(2, parts, rows, span).transpose(1, 0, 2, 3)
    table = np.zeros((parts, 2, padded, span), np.float32)
    table[:, :, :rows] = waves
    return table.astype(jnp.bfloat16)


def nt_dot(a, b):
    return lax.dot_general(a, b, (((1,), (1,)), ((), ())), preferred_element_type=F32)


def kernel(
    sizes,
    u_ref,
    v_ref,
    t_ref,
    keep_ref,
    table_ref,
    cosine_ref,
    depth_ref,
    target_ref,
    psi_ref,
    heat_ref,
    moment_ref,
    penalty_ref,
    raw,
    keep,
    masked,
    doubled,
    arrived,
    table,
    given,
    returned,
    zonal_mine,
    zonal_theirs,
    mean_mine,
    gathered,
    stream_buf,
    load_sem,
    table_sem,
    field_send,
    field_recv,
    back_send,
    back_recv,
    zonal_sem,
    mean_send,
    mean_recv,
):
    bands, batch, levels, span, rows, rows_sent, groups, lev_ways = sizes
    columns = batch * levels
    padded_rows = table.shape[2]
    half, mid = bands // 2, bands % 2
    half_columns = columns // 2
    slab = mean_mine.shape[0] // 2
    me = lax.axis_index("lon")
    other = 1 - me
    mine = lax.axis_index("lat") * lev_ways + lax.axis_index("lev")
    partner = {"lon": other}
    norm_factor = 2.0 / (4.0 * span * span)

    their_rows = [other * (half + mid) + i for i in range(half)]
    my_rows = [me * (half + mid) + i for i in range(half)]
    order = ([half] if mid else []) + their_rows + my_rows

    loads = []
    for place, row in enumerate(order):
        loads.append(
            [
                pltpu.make_async_copy(keep_ref.at[row], keep.at[row], load_sem.at[place, 3]),
                pltpu.make_async_copy(u_ref.at[row], raw.at[row, 0], load_sem.at[place, 0]),
                pltpu.make_async_copy(v_ref.at[row], raw.at[row, 1], load_sem.at[place, 1]),
                pltpu.make_async_copy(t_ref.at[row], raw.at[row, 2], load_sem.at[place, 2]),
            ]
        )
        for copy in loads[-1]:
            copy.start()
    table_load = pltpu.make_async_copy(table_ref, table, table_sem)
    table_load.start()

    def mask_row(place):
        row = order[place]
        for copy in loads[place]:
            copy.wait()
        ones = keep[row].astype(F32).astype(BF16)
        for field in range(3):
            for sample in range(batch):
                part = pl.ds(sample * levels, levels)
                masked[row, field, part, :] = raw[row, field, part, :] * ones

    def remote(src, dst, send, recv):
        return pltpu.make_async_remote_copy(
            src_ref=src,
            dst_ref=dst,
            send_sem=send,
            recv_sem=recv,
            device_id=partner,
            device_id_type=pl.DeviceIdType.MESH,
        )

    field_copies = []

    def send_row(piece, place):
        row = order[place]
        if mid and piece == 0:
            away = pl.ds(pl.multiple_of(other * half_columns, half_columns), half_columns)
            copies = [
                remote(
                    masked.at[row, field, away, :],
                    arrived.at[piece, field, pl.ds(0, half_columns), :],
                    field_send.at[piece, field],
                    field_recv.at[piece, field],
                )
                for field in range(3)
            ]
        else:
            copies = [
                remote(
                    masked.at[row, field],
                    arrived.at[piece, field],
                    field_send.at[piece, field],
                    field_recv.at[piece, field],
                )
                for field in range(3)
            ]
        for copy in copies:
            copy.start()
        field_copies.append(copies)

    early = min(mid + 1, mid + half)
    for place in range(early):
        mask_row(place)
        send_row(place, place)
    for place in range(early, len(order)):
        mask_row(place)

    ones_row = jnp.ones((8, span), BF16)
    zonal_mine[...] = jnp.zeros_like(zonal_mine)
    for row in range(bands):
        zonal_mine[pl.ds(row, 1), :] = nt_dot(ones_row, masked[row, 1])[0:1]
        counts = nt_dot(ones_row, keep[row].astype(F32).astype(BF16))[0:1]
        zonal_mine[pl.ds(slab + row, 1), :] = jnp.concatenate([counts] * batch, axis=1)
    zonal_copy = remote(zonal_mine, zonal_theirs, zonal_sem.at[0], zonal_sem.at[1])
    zonal_copy.start()
    for place in range(early, mid + half):
        send_row(place, place)

    if mid:
        here = pl.ds(pl.multiple_of(me * half_columns, half_columns), half_columns)
        for field in range(3):
            own = masked[half, field, here, :]
            doubled[field, pl.ds(0, half_columns), :] = own
            doubled[field, pl.ds(half_columns, half_columns), :] = own
    table_load.wait()

    row_index = lax.broadcasted_iota(jnp.int32, (padded_rows, 1), 0)
    left_lanes = lax.broadcasted_iota(jnp.int32, (1, columns), 1) < half_columns
    back_copies = []

    def transform(part, near, far):
        parity = (row_index + 1 + part * rows) % 2
        sign = (1 - 2 * parity).astype(F32)
        pieces = []
        for trig in range(2):
            wave = table[part, trig]
            pieces.append([nt_dot(wave, near(f)) + sign * nt_dot(wave, far(f)) for f in range(3)])
        (uc, vc, tc), (us, vs, ts) = pieces
        return norm_factor * (vc * tc + vs * ts), norm_factor * (uc * vc + us * vs)

    def process(piece):
        for copy in field_copies[piece]:
            copy.wait_recv()
        is_mid = mid and piece == 0
        if is_mid:
            row = half
            for field in range(3):
                arrived[piece, field, pl.ds(half_columns, half_columns), :] = arrived[
                    piece, field, pl.ds(0, half_columns), :
                ]
            near = lambda f: doubled[f]
        else:
            row = my_rows[piece - mid]
            near = lambda f: masked[row, f]
        far = lambda f: arrived[piece, f]
        heat, moment = transform(other, near, far)
        if is_mid:
            given[piece, 0] = jnp.where(left_lanes, heat, moment).astype(BF16)
        else:
            given[piece, 0] = heat.astype(BF16)
            given[piece, 1] = moment.astype(BF16)
        sent = pl.ds(0, rows_sent)
        copies = [
            remote(
                given.at[piece, which, sent, :],
                returned.at[piece, which, sent, :],
                back_send.at[piece, which],
                back_recv.at[piece, which],
            )
            for which in range(1 if is_mid else 2)
        ]
        for copy in copies:
            copy.start()
        back_copies.append(copies)
        heat, moment = transform(me, near, far)
        heat_ref[row] = heat[:rows]
        moment_ref[row] = moment[:rows]

    def mean_to(step):
        peer = (mine + step) % groups
        return pltpu.make_async_remote_copy(
            src_ref=mean_mine,
            dst_ref=gathered.at[mine],
            send_sem=mean_send.at[step],
            recv_sem=mean_recv.at[mine],
            device_id={"lat": peer // lev_ways, "lev": peer % lev_ways},
            device_id_type=pl.DeviceIdType.MESH,
        )

    def mean_from(step):
        peer = (mine + step) % groups
        return pltpu.make_async_remote_copy(
            src_ref=mean_mine,
            dst_ref=gathered.at[peer],
            send_sem=mean_send.at[step],
            recv_sem=mean_recv.at[peer],
            device_id={"lat": peer // lev_ways, "lev": peer % lev_ways},
            device_id_type=pl.DeviceIdType.MESH,
        )

    def share_means():
        zonal_copy.wait_recv()
        total = zonal_mine[...] + zonal_theirs[...]
        mean_mine[...] = jnp.zeros_like(mean_mine)
        mean_mine[pl.ds(0, slab), :] = total[:slab] / jnp.maximum(total[slab:], 1.0)
        target = jnp.concatenate([target_ref[:, b, :] for b in range(batch)], axis=1)
        mean_mine[pl.ds(slab, bands), :] = target
        gathered[mine] = mean_mine[...]

        def start(step, carry):
            mean_to(step).start()
            return carry

        lax.fori_loop(1, groups, start, 0)

    def finish_stream():
        def arrive(step, carry):
            mean_from(step).wait_recv()
            return carry

        lax.fori_loop(1, groups, arrive, 0)
        height = groups * slab
        cosine = cosine_ref[...]
        depth = jnp.concatenate([depth_ref[...]] * batch, axis=1)
        mean = gathered[:, 0:slab, :].reshape(height, columns)
        target = gathered[:, slab : 2 * slab, :].reshape(height, columns)
        stream = mean * cosine * depth
        lane = lax.broadcasted_iota(jnp.int32, (height, columns), 1) % levels
        line = lax.broadcasted_iota(jnp.int32, (height, columns), 0)
        step = 1
        while step < levels:
            stream = stream + jnp.where(lane >= step, pltpu.roll(stream, step, 1), 0.0)
            step *= 2
        step = 1
        while step < height:
            stream = stream + jnp.where(line >= step, pltpu.roll(stream, step, 0), 0.0)
            step *= 2
        peak = jnp.max(jnp.abs(stream))
        stream = stream / (peak + epsilon)
        misfit = jnp.sum(cosine * (stream - target) ** 2)
        penalty_ref[...] = jnp.full((1, 1), misfit / (columns * bands * groups), F32)
        stream_buf[...] = stream
        own = stream_buf[pl.ds(pl.multiple_of(mine * slab, slab), slab), :][:bands]
        for b in range(batch):
            psi_ref[:, b, :] = own[:, b * levels : (b + 1) * levels]

    pieces = mid + half
    for piece in range(pieces):
        if piece == min(1, pieces - 1):
            share_means()
        if piece == pieces - 1:
            finish_stream()
        process(piece)

    for piece in range(pieces):
        for copy in back_copies[piece]:
            copy.wait_recv()
        if mid and piece == 0:
            both = returned[piece, 0].astype(F32)[:rows]
            turned = pltpu.roll(both, half_columns, 1)
            mine_lanes = (lax.broadcasted_iota(jnp.int32, (1, columns), 1) // half_columns) == me
            first = me == 0
            heat_far = jnp.where(first, turned, both)
            moment_far = jnp.where(first, both, turned)
            heat_ref[half] = jnp.where(mine_lanes, heat_ref[half], heat_far)
            moment_ref[half] = jnp.where(mine_lanes, moment_ref[half], moment_far)
        else:
            row = their_rows[piece - mid]
            heat_ref[row] = returned[piece, 0].astype(F32)[:rows]
            moment_ref[row] = returned[piece, 1].astype(F32)[:rows]

    for copies in field_copies + back_copies:
        for copy in copies:
            copy.wait_send()
    zonal_copy.wait_send()

    def sent_all(step, carry):
        mean_to(step).wait_send()
        return carry

    lax.fori_loop(1, groups, sent_all, 0)


def per_device(mesh_shape, u, v, t, keep, depth, target):
    bands, batch, levels, span = v.shape
    lon_ways = mesh_shape["lon"]
    assert lon_ways == 2
    lev_ways = mesh_shape["lev"]
    groups = mesh_shape["lat"] * lev_ways
    rows = HARMONIC_ORDERS // lon_ways
    padded = round_up(rows, 128)
    rows_sent = round_up(rows, 16)
    columns = batch * levels
    half, mid = bands // 2, bands % 2
    pieces = half + mid
    slab = round_up(bands, 8)
    nlat = bands * groups
    table = jnp.asarray(wave_table(span * lon_ways, lon_ways, rows, padded, span))
    latitude = ((np.arange(nlat).astype(np.float32) + np.float32(0.5)) / np.float32(nlat) - np.float32(0.5)) * np.float32(math.pi)
    cosine = np.zeros((groups, slab, 1), np.float32)
    cosine[:, :bands, 0] = np.cos(latitude).reshape(groups, bands)
    cosine = jnp.asarray(np.broadcast_to(cosine.reshape(groups * slab, 1), (groups * slab, columns)).copy())
    fields = [x.reshape(bands, columns, span) for x in (u, v, t)]
    sizes = (bands, batch, levels, span, rows, rows_sent, groups, lev_ways)
    anywhere = pl.BlockSpec(memory_space=pl.ANY)
    inside = pl.BlockSpec(memory_space=pltpu.VMEM)
    psi, heat, moment, penalty = pl.pallas_call(
        functools.partial(kernel, sizes),
        out_shape=(
            jax.ShapeDtypeStruct((bands, batch, levels), F32),
            jax.ShapeDtypeStruct((bands, rows, columns), F32),
            jax.ShapeDtypeStruct((bands, rows, columns), F32),
            jax.ShapeDtypeStruct((1, 1), F32),
        ),
        in_specs=[anywhere] * 5 + [inside] * 3,
        out_specs=(inside,) * 4,
        scratch_shapes=[
            pltpu.VMEM((bands, 3, columns, span), BF16),
            pltpu.VMEM((bands, levels, span), jnp.int32),
            pltpu.VMEM((bands, 3, columns, span), BF16),
            pltpu.VMEM((3, columns, span), BF16),
            pltpu.VMEM((pieces, 3, columns, span), BF16),
            pltpu.VMEM(table.shape, BF16),
            pltpu.VMEM((pieces, 2, padded, columns), BF16),
            pltpu.VMEM((pieces, 2, padded, columns), BF16),
            pltpu.VMEM((2 * slab, columns), F32),
            pltpu.VMEM((2 * slab, columns), F32),
            pltpu.VMEM((2 * slab, columns), F32),
            pltpu.VMEM((groups, 2 * slab, columns), F32),
            pltpu.VMEM((groups * slab, columns), F32),
            pltpu.SemaphoreType.DMA((bands, 4)),
            pltpu.SemaphoreType.DMA,
            pltpu.SemaphoreType.DMA((pieces, 3)),
            pltpu.SemaphoreType.DMA((pieces, 3)),
            pltpu.SemaphoreType.DMA((pieces, 2)),
            pltpu.SemaphoreType.DMA((pieces, 2)),
            pltpu.SemaphoreType.DMA((2,)),
            pltpu.SemaphoreType.DMA((groups,)),
            pltpu.SemaphoreType.DMA((groups,)),
        ],
        compiler_params=pltpu.CompilerParams(
            has_side_effects=True, vmem_limit_bytes=56 * 1024 * 1024
        ),
    )(*fields, keep, table, cosine, depth.reshape(1, levels), target)
    return psi, heat.transpose(1, 0, 2), moment.transpose(1, 0, 2), penalty.reshape(())


def solution(mesh):
    banded = ("lat", "lev")
    placed = (
        P(banded, None, None, "lon"),
        P(banded, None, None, "lon"),
        P(banded, None, None, "lon"),
        P(banded, None, "lon"),
        P(),
        P(banded, None, None),
    )
    return jax.shard_map(
        functools.partial(per_device, dict(mesh.shape)),
        mesh=mesh,
        in_specs=placed,
        out_specs=(P(banded, None, None), P("lon", banded, None), P("lon", banded, None), P()),
        check_vma=False,
    )
```

time: 154 us -> 63.1 us (0.41)
  blocking collectives: 91.9 us -> 0 us
  Pallas kernels: 0 us -> 56.1 us
  matrix products: 25.1 us -> 0 us
  between operations: 16.6 us -> 2.32 us
  other arithmetic: 12.6 us -> 0 us
  local copies, waits for them, and re-layouts: 6.79 us -> 4.47 us
    pallas_call x0 -> x1, Pallas kernels: none -> 56.1 us  [per_device(): pl.pallas_call(functools.partial(kernel, sizes), out_shape=(jax.ShapeDtyp...]
    psum x2 -> x0, blocking collectives: 39.7 us -> none  [the longest x1 30.1 us: per_device(): budget_penalty = lax.psum(local_misfit, ('lat', 'lev')) / cell_count]
    pmax x1 -> x0, blocking collectives: 30.4 us -> none  [per_device(): peak_value = lax.pmax(local_peak, ('lat', 'lev'))]
    dot_general x1 -> x0, matrix products: 25.1 us -> none  [per_device(): lax.dot_general(waves_table, lax.all_gather(joined_arrays, 'lon', axis=3,...]
    all_gather x1 -> x0, blocking collectives: 21.7 us -> none  [entering(): pieces = lax.all_gather(value, axis)]
    unnamed x4 -> x5, local copies, waits for them, and re-layouts: 0.01 us -> 4.47 us
    reduce_sum x3 -> x0, other arithmetic: 4.14 us -> none  [the longest x1 1.53 us: per_device(): zonal_v = jnp.sum(screened_northward_speed, axis=3, dtype=jnp.float32)]
    another operation x3 -> x0, other arithmetic: 4.04 us -> none  [the longest x1 3.02 us: per_device(): jnp.stack([screened_eastward_speed, screened_northward_speed, screened_th...]
  transfers between devices with their start and end apart: 1 -> 0, of which waited for: 0 -> 0; matrix products, arithmetic and copies ran while one was open for 2% -> 0% of each run, Pallas kernels for 0% -> 0%
where the time goes in v1:
time: 63.1 us; the launch traced here: 62.9 us
  Pallas kernels  56.1 us (89%)
  local copies, waits for them, and re-layouts  4.47 us (7%)
  between operations  2.32 us (4%)
    pallas_call x1, Pallas kernels, per_device(): pl.pallas_call(functools.partial(kernel, sizes), out_shape=(jax.ShapeDtyp...  56.1 us
    unnamed x5, local copies, waits for them, and re-layouts  4.47 us

profile of v1, /device:TPU:0, one launch (start us, length us, event | category | flops | bytes accessed | tf_op | source)
XLA Modules:
  0.0 62.9 jit_solution(7756191180354356578)
XLA Ops:
  0.6 56.1 %shard_map.111 = (f32[5,4,32]{2,1,0:T(4,128)}, f32[5,360,128]{2,1,0:T(8,128)}, f32[5,360,128]{2,1,0:T(8,128)}, f32[1,1]{1,0:T(1,128)}) custom-call(bf16[5,128,720]{2,1,0:T(8,128)(2,1)} %bitcast.7, bf16[5,128,720]{2,1,0:T(8,128)(2,1)} %bitcast.8, bf16[5,128,720]{2,1,0:T(8,128)(2,1)} %bitcast.9, s32[5,32,720]{2,1,0:T(8,128)} %keep_ref.1, ...), custom_call_target="tpu_custom_call" | custom-call | tf_op jit(solution)/shard_map/pallas_call | solution.py:360
  56.7 0.0 copy-start
  56.7 1.4 %copy.16 = f32[5,4,32]{2,1,0:T(4,128)} copy(f32[5,4,32]{2,1,0:T(4,128)} %get-tuple-element.16) | data formatting | bytes 5120
  58.1 2.2 %copy.17 = f32[360,5,128]{2,0,1:T(8,128)} copy(f32[360,5,128]{2,0,1:T(8,128)} %bitcast.11) | data formatting | bytes 1843200
  60.3 0.0 copy-done
  60.3 0.9 %copy.18 = f32[360,5,128]{2,0,1:T(8,128)} copy(f32[360,5,128]{2,0,1:T(8,128)S(1)} %bitcast.10) | data formatting | bytes 1843200
Async XLA Ops:
  56.7 3.6 %copy-start = (f32[5,360,128]{2,1,0:T(8,128)S(1)}, f32[5,360,128]{2,1,0:T(8,128)}, u32[]{:S(2)}) copy-start(f32[5,360,128]{2,1,0:T(8,128)} %get-tuple-element.10) | copy-start | bytes 2764804

commit v2 on v1

--- a/solution.py
+++ b/solution.py
@@ -45,17 +45,17 @@
     depth_ref,
     target_ref,
     psi_ref,
-    heat_ref,
-    moment_ref,
+    own_ref,
+    returned,
     penalty_ref,
     raw,
     keep,
     masked,
     doubled,
+    packed,
     arrived,
     table,
     given,
-    returned,
     zonal_mine,
     zonal_theirs,
     mean_mine,
@@ -82,6 +82,21 @@
     mine = lax.axis_index("lat") * lev_ways + lax.axis_index("lev")
     partner = {"lon": other}
     norm_factor = 2.0 / (4.0 * span * span)
+    body = span // 128 * 128
+    tail = span - body
+    whole = lambda step: (mine + step) % groups
+    place_of = lambda peer: {"lat": peer // lev_ways, "lev": peer % lev_ways}
+
+    barrier = pltpu.get_barrier_semaphore()
+    pl.semaphore_signal(barrier, inc=1, device_id=partner, device_id_type=pl.DeviceIdType.MESH)
+
+    def greet(step, carry):
+        pl.semaphore_signal(
+            barrier, inc=1, device_id=place_of(whole(step)), device_id_type=pl.DeviceIdType.MESH
+        )
+        return carry
+
+    lax.fori_loop(1, groups, greet, 0)
 
     their_rows = [other * (half + mid) + i for i in range(half)]
     my_rows = [me * (half + mid) + i for i in range(half)]
@@ -124,32 +139,37 @@
 
     field_copies = []
 
-    def send_row(piece, place):
+    def pack_row(piece, place):
         row = order[place]
         if mid and piece == 0:
             away = pl.ds(pl.multiple_of(other * half_columns, half_columns), half_columns)
-            copies = [
-                remote(
-                    masked.at[row, field, away, :],
-                    arrived.at[piece, field, pl.ds(0, half_columns), :],
-                    field_send.at[piece, field],
-                    field_recv.at[piece, field],
-                )
-                for field in range(3)
-            ]
+            here = pl.ds(0, half_columns)
         else:
-            copies = [
-                remote(
-                    masked.at[row, field],
-                    arrived.at[piece, field],
-                    field_send.at[piece, field],
-                    field_recv.at[piece, field],
-                )
-                for field in range(3)
-            ]
-        for copy in copies:
-            copy.start()
-        field_copies.append(copies)
+            away = here = pl.ds(0, columns)
+        ends = []
+        for field in range(3):
+            packed[piece, here, pl.ds(field * body, body)] = masked[row, field, away, pl.ds(0, body)]
+            ends.append(masked[row, field, away, pl.ds(body, tail)])
+        packed[piece, here, pl.ds(3 * body, 3 * tail)] = jnp.concatenate(ends, axis=1)
+        return here
+
+    def send_row(piece, place):
+        here = pack_row(piece, place)
+        if place == 0:
+            pl.semaphore_wait(barrier, groups)
+        copy = remote(
+            packed.at[piece, here, :],
+            arrived.at[piece, here, :],
+            field_send.at[piece],
+            field_recv.at[piece],
+        )
+        copy.start()
+        field_copies.append([copy])
+
+    def far_field(piece, field):
+        bulk = arrived[piece, :, pl.ds(field * body, body)]
+        end = arrived[piece, :, pl.ds(3 * body + field * tail, tail)]
+        return jnp.concatenate([bulk, end], axis=1)
 
     early = min(mid + 1, mid + half)
     for place in range(early):
@@ -196,16 +216,14 @@
             copy.wait_recv()
         is_mid = mid and piece == 0
         if is_mid:
-            row = half
-            for field in range(3):
-                arrived[piece, field, pl.ds(half_columns, half_columns), :] = arrived[
-                    piece, field, pl.ds(0, half_columns), :
-                ]
+            arrived[piece, pl.ds(half_columns, half_columns), :] = arrived[
+                piece, pl.ds(0, half_columns), :
+            ]
             near = lambda f: doubled[f]
         else:
             row = my_rows[piece - mid]
             near = lambda f: masked[row, f]
-        far = lambda f: arrived[piece, f]
+        far = lambda f: far_field(piece, f)
         heat, moment = transform(other, near, far)
         if is_mid:
             given[piece, 0] = jnp.where(left_lanes, heat, moment).astype(BF16)
@@ -226,28 +244,28 @@
             copy.start()
         back_copies.append(copies)
         heat, moment = transform(me, near, far)
-        heat_ref[row] = heat[:rows]
-        moment_ref[row] = moment[:rows]
+        own_ref[piece, 0] = heat[:rows]
+        own_ref[piece, 1] = moment[:rows]
 
     def mean_to(step):
-        peer = (mine + step) % groups
+        peer = whole(step)
         return pltpu.make_async_remote_copy(
             src_ref=mean_mine,
             dst_ref=gathered.at[mine],
             send_sem=mean_send.at[step],
             recv_sem=mean_recv.at[mine],
-            device_id={"lat": peer // lev_ways, "lev": peer % lev_ways},
+            device_id=place_of(peer),
             device_id_type=pl.DeviceIdType.MESH,
         )
 
     def mean_from(step):
-        peer = (mine + step) % groups
+        peer = whole(step)
         return pltpu.make_async_remote_copy(
             src_ref=mean_mine,
             dst_ref=gathered.at[peer],
             send_sem=mean_send.at[step],
             recv_sem=mean_recv.at[peer],
-            device_id={"lat": peer // lev_ways, "lev": peer % lev_ways},
+            device_id=place_of(peer),
             device_id_type=pl.DeviceIdType.MESH,
         )
 
@@ -305,23 +323,9 @@
             finish_stream()
         process(piece)
 
-    for piece in range(pieces):
-        for copy in back_copies[piece]:
+    for copies in back_copies:
+        for copy in copies:
             copy.wait_recv()
-        if mid and piece == 0:
-            both = returned[piece, 0].astype(F32)[:rows]
-            turned = pltpu.roll(both, half_columns, 1)
-            mine_lanes = (lax.broadcasted_iota(jnp.int32, (1, columns), 1) // half_columns) == me
-            first = me == 0
-            heat_far = jnp.where(first, turned, both)
-            moment_far = jnp.where(first, both, turned)
-            heat_ref[half] = jnp.where(mine_lanes, heat_ref[half], heat_far)
-            moment_ref[half] = jnp.where(mine_lanes, moment_ref[half], moment_far)
-        else:
-            row = their_rows[piece - mid]
-            heat_ref[row] = returned[piece, 0].astype(F32)[:rows]
-            moment_ref[row] = returned[piece, 1].astype(F32)[:rows]
-
     for copies in field_copies + back_copies:
         for copy in copies:
             copy.wait_send()
@@ -332,6 +336,56 @@
         return carry
 
     lax.fori_loop(1, groups, sent_all, 0)
+
+
+def assemble(sizes, psi_in, own_ref, returned, penalty_in, psi_ref, heat_ref, moment_ref, penalty_ref, stage, sems):
+    bands, batch, levels, rows = sizes
+    columns = batch * levels
+    half, mid = bands // 2, bands % 2
+    half_columns = columns // 2
+    me = lax.axis_index("lon")
+    other = 1 - me
+    copies = []
+
+    def put(row, slot, heat, moment):
+        stage[slot, 0] = heat
+        stage[slot, 1] = moment
+        for which, out in enumerate((heat_ref, moment_ref)):
+            copy = pltpu.make_async_copy(stage.at[slot, which], out.at[row], sems.at[slot, which])
+            copy.start()
+            copies.append(copy)
+
+    for i in range(half):
+        piece = mid + i
+        for which, out in enumerate((heat_ref, moment_ref)):
+            copy = pltpu.make_async_copy(
+                own_ref.at[piece, which], out.at[me * (half + mid) + i], sems.at[half + mid + i, which]
+            )
+            copy.start()
+            copies.append(copy)
+    for i in range(half):
+        piece = mid + i
+        put(
+            other * (half + mid) + i,
+            piece,
+            returned[piece, 0, :rows].astype(F32),
+            returned[piece, 1, :rows].astype(F32),
+        )
+    if mid:
+        both = returned[0, 0, :rows].astype(F32)
+        turned = pltpu.roll(both, half_columns, 1)
+        mine_lanes = (lax.broadcasted_iota(jnp.int32, (1, columns), 1) // half_columns) == me
+        first = me == 0
+        put(
+            half,
+            0,
+            jnp.where(mine_lanes, own_ref[0, 0], jnp.where(first, turned, both)),
+            jnp.where(mine_lanes, own_ref[0, 1], jnp.where(first, both, turned)),
+        )
+    psi_ref[...] = psi_in[...]
+    penalty_ref[...] = penalty_in[...]
+    for copy in copies:
+        copy.wait()
 
 
 def per_device(mesh_shape, u, v, t, keep, depth, target):
@@ -357,24 +411,27 @@
     sizes = (bands, batch, levels, span, rows, rows_sent, groups, lev_ways)
     anywhere = pl.BlockSpec(memory_space=pl.ANY)
     inside = pl.BlockSpec(memory_space=pltpu.VMEM)
-    psi, heat, moment, penalty = pl.pallas_call(
+    in_hbm = pl.BlockSpec(memory_space=pltpu.MemorySpace.HBM)
+    body = span // 128 * 128
+    lanes = 3 * body + round_up(3 * (span - body), 128)
+    mid_results = pl.pallas_call(
         functools.partial(kernel, sizes),
         out_shape=(
             jax.ShapeDtypeStruct((bands, batch, levels), F32),
-            jax.ShapeDtypeStruct((bands, rows, columns), F32),
-            jax.ShapeDtypeStruct((bands, rows, columns), F32),
+            jax.ShapeDtypeStruct((pieces, 2, rows, columns), F32),
+            jax.ShapeDtypeStruct((pieces, 2, padded, columns), BF16),
             jax.ShapeDtypeStruct((1, 1), F32),
         ),
-        in_specs=[anywhere] * 5 + [inside] * 3,
+        in_specs=[in_hbm] * 5 + [inside] * 3,
         out_specs=(inside,) * 4,
         scratch_shapes=[
             pltpu.VMEM((bands, 3, columns, span), BF16),
             pltpu.VMEM((bands, levels, span), jnp.int32),
             pltpu.VMEM((bands, 3, columns, span), BF16),
             pltpu.VMEM((3, columns, span), BF16),
-            pltpu.VMEM((pieces, 3, columns, span), BF16),
+            pltpu.VMEM((pieces, columns, lanes), BF16),
+            pltpu.VMEM((pieces, columns, lanes), BF16),
             pltpu.VMEM(table.shape, BF16),
-            pltpu.VMEM((pieces, 2, padded, columns), BF16),
             pltpu.VMEM((pieces, 2, padded, columns), BF16),
             pltpu.VMEM((2 * slab, columns), F32),
             pltpu.VMEM((2 * slab, columns), F32),
@@ -383,8 +440,8 @@
             pltpu.VMEM((groups * slab, columns), F32),
             pltpu.SemaphoreType.DMA((bands, 4)),
             pltpu.SemaphoreType.DMA,
-            pltpu.SemaphoreType.DMA((pieces, 3)),
-            pltpu.SemaphoreType.DMA((pieces, 3)),
+            pltpu.SemaphoreType.DMA((pieces,)),
+            pltpu.SemaphoreType.DMA((pieces,)),
             pltpu.SemaphoreType.DMA((pieces, 2)),
             pltpu.SemaphoreType.DMA((pieces, 2)),
             pltpu.SemaphoreType.DMA((2,)),
@@ -392,9 +449,25 @@
             pltpu.SemaphoreType.DMA((groups,)),
         ],
         compiler_params=pltpu.CompilerParams(
-            has_side_effects=True, vmem_limit_bytes=56 * 1024 * 1024
+            collective_id=0, has_side_effects=True, vmem_limit_bytes=32 * 1024 * 1024
         ),
     )(*fields, keep, table, cosine, depth.reshape(1, levels), target)
+    psi, heat, moment, penalty = pl.pallas_call(
+        functools.partial(assemble, (bands, batch, levels, rows)),
+        out_shape=(
+            jax.ShapeDtypeStruct((bands, batch, levels), F32),
+            jax.ShapeDtypeStruct((bands, rows, columns), F32),
+            jax.ShapeDtypeStruct((bands, rows, columns), F32),
+            jax.ShapeDtypeStruct((1, 1), F32),
+        ),
+        in_specs=[inside] * 4,
+        out_specs=(inside, anywhere, anywhere, inside),
+        scratch_shapes=[
+            pltpu.VMEM((pieces, 2, rows, columns), F32),
+            pltpu.SemaphoreType.DMA((pieces + half, 2)),
+        ],
+        compiler_params=pltpu.CompilerParams(vmem_limit_bytes=8 * 1024 * 1024),
+    )(*mid_results)
     return psi, heat.transpose(1, 0, 2), moment.transpose(1, 0, 2), penalty.reshape(())
 
 

time: 63.1 us -> 62 us (0.983)
  local copies, waits for them, and re-layouts: 4.47 us -> 8.49 us
  Pallas kernels: 56.1 us -> 52.5 us
  between operations: 2.32 us -> 0.66 us
    pallas_call x1, Pallas kernels: 56.1 us -> 49.9 us  [per_device(): pl.pallas_call(functools.partial(kernel, sizes), out_shape=(jax.ShapeDtyp...]
    unnamed x5 -> x16, local copies, waits for them, and re-layouts: 4.47 us -> 8.49 us
    pallas_call x0 -> x1, Pallas kernels: none -> 2.54 us  [per_device(): pl.pallas_call(functools.partial(assemble, (bands, batch, levels, rows)),...]
where the time goes in v2:
time: 62 us; the launch traced here: 61.6 us
  Pallas kernels  52.5 us (85%)
  local copies, waits for them, and re-layouts  8.49 us (14%)
  between operations  0.66 us (1%)
    pallas_call x1, Pallas kernels, per_device(): pl.pallas_call(functools.partial(kernel, sizes), out_shape=(jax.ShapeDtyp...  49.9 us
    unnamed x16, local copies, waits for them, and re-layouts  8.49 us
    pallas_call x1, Pallas kernels, per_device(): pl.pallas_call(functools.partial(assemble, (bands, batch, levels, rows)),...  2.54 us

profile of v2, /device:TPU:0, one launch (start us, length us, event | category | flops | bytes accessed | tf_op | source)
XLA Modules:
  0.0 61.6 jit_solution(2398364004240907540)
XLA Ops:
  0.6 0.0 copy-start
  0.6 1.7 %copy-done = bf16[2,2,384,720]{3,2,1,0:T(8,128)(2,1)S(1)} copy-done((bf16[2,2,384,720]{3,2,1,0:T(8,128)(2,1)S(1)}, bf16[2,2,384,720]{3,2,1,0:T(8,128)(2,1)}, u32[]{:S(2)}) %copy-start) | copy-done | bytes 2211864
  2.3 0.0 copy-start.1
  2.3 1.2 %copy-done.1 = bf16[5,4,32,720]{3,2,1,0:T(8,128)(2,1)S(1)} copy-done((bf16[5,4,32,720]{3,2,1,0:T(8,128)(2,1)S(1)}, bf16[5,4,32,720]{3,2,1,0:T(8,128)(2,1)}, u32[]{:S(2)}) %copy-start.1) | copy-done | bytes 921624
  3.5 0.0 copy-start.2
  3.5 1.2 %copy-done.2 = bf16[5,4,32,720]{3,2,1,0:T(8,128)(2,1)S(1)} copy-done((bf16[5,4,32,720]{3,2,1,0:T(8,128)(2,1)S(1)}, bf16[5,4,32,720]{3,2,1,0:T(8,128)(2,1)}, u32[]{:S(2)}) %copy-start.2) | copy-done | bytes 921624
  4.7 0.0 copy-start.3
  4.7 1.2 %copy-done.3 = bf16[5,4,32,720]{3,2,1,0:T(8,128)(2,1)S(1)} copy-done((bf16[5,4,32,720]{3,2,1,0:T(8,128)(2,1)S(1)}, bf16[5,4,32,720]{3,2,1,0:T(8,128)(2,1)}, u32[]{:S(2)}) %copy-start.3) | copy-done | bytes 921624
  5.9 0.0 copy-start.4
  5.9 1.0 %copy-done.4 = s32[5,32,720]{2,1,0:T(8,128)S(1)} copy-done((s32[5,32,720]{2,1,0:T(8,128)S(1)}, s32[5,32,720]{2,1,0:T(8,128)}, u32[]{:S(2)}) %copy-start.4) | copy-done | bytes 460824
  6.9 0.0 copy-start.5
  6.9 0.8 %copy-done.5 = f32[128,128]{1,0:T(8,128)S(1)} copy-done((f32[128,128]{1,0:T(8,128)S(1)}, f32[128,128]{1,0:T(8,128)}, u32[]{:S(2)}) %copy-start.5) | copy-done | bytes 65560
  7.8 0.0 copy-start.6
  7.8 0.7 %copy-done.6 = f32[5,4,32]{2,1,0:T(4,128)S(1)} copy-done((f32[5,4,32]{2,1,0:T(4,128)S(1)}, f32[5,4,32]{2,1,0:T(4,128)}, u32[]{:S(2)}) %copy-start.6) | copy-done | bytes 2584
  8.5 0.0 copy-start.7
  8.5 0.7 %copy-done.7 = f32[32]{0:T(128)S(1)} copy-done((f32[32]{0:T(128)S(1)}, f32[32]{0:T(128)}, u32[]{:S(2)}) %copy-start.7) | copy-done | bytes 152
  9.1 49.9 %shard_map.111 = (f32[5,4,32]{2,1,0:T(4,128)S(1)}, f32[3,2,360,128]{3,2,1,0:T(8,128)S(1)}, bf16[3,2,384,128]{3,2,1,0:T(8,128)(2,1)S(1)}, f32[1,1]{1,0:T(1,128)}) custom-call(bf16[5,128,720]{2,1,0:T(8,128)(2,1)S(1)} %bitcast.7, bf16[5,128,720]{2,1,0:T(8,128)(2,1)S(1)} %bitcast.8, bf16[5,128,720]{2,1,0:T(8,128)(2,1)S(1)} %bitcast.9, ...), custom_call_target="tpu_custom_call" | custom-call | tf_op jit(solution)/shard_map/pallas_call | solution.py:417
  59.1 2.5 %shard_map.112 = (f32[5,4,32]{2,1,0:T(4,128)}, f32[5,360,128]{2,1,0:T(8,128)}, f32[5,360,128]{2,1,0:T(8,128)}, f32[1,1]{1,0:T(1,128)}) custom-call(f32[5,4,32]{2,1,0:T(4,128)S(1)} %get-tuple-element.12.psi_in, f32[3,2,360,128]{3,2,1,0:T(8,128)S(1)} %get-tuple-element.13.own_ref, bf16[3,2,384,128]{3,2,1,0:T(8,128)(2,1)S(1)} %get-tuple-element.14.returned, ...), custom_call_target="tpu_custom_call" | custom-call | tf_op jit(solution)/shard_map/pallas_call | solution.py:455
Async XLA Ops:
  0.6 1.7 %copy-start = (bf16[2,2,384,720]{3,2,1,0:T(8,128)(2,1)S(1)}, bf16[2,2,384,720]{3,2,1,0:T(8,128)(2,1)}, u32[]{:S(2)}) copy-start(bf16[2,2,384,720]{3,2,1,0:T(8,128)(2,1)} %constant.4.clone.table_ref) | copy-start | bytes 6635524
  2.3 1.2 %copy-start.1 = (bf16[5,4,32,720]{3,2,1,0:T(8,128)(2,1)S(1)}, bf16[5,4,32,720]{3,2,1,0:T(8,128)(2,1)}, u32[]{:S(2)}) copy-start(bf16[5,4,32,720]{3,2,1,0:T(8,128)(2,1)} %param.8) | copy-start | bytes 2764804
  3.5 1.2 %copy-start.2 = (bf16[5,4,32,720]{3,2,1,0:T(8,128)(2,1)S(1)}, bf16[5,4,32,720]{3,2,1,0:T(8,128)(2,1)}, u32[]{:S(2)}) copy-start(bf16[5,4,32,720]{3,2,1,0:T(8,128)(2,1)} %param.9) | copy-start | bytes 2764804
  4.7 1.2 %copy-start.3 = (bf16[5,4,32,720]{3,2,1,0:T(8,128)(2,1)S(1)}, bf16[5,4,32,720]{3,2,1,0:T(8,128)(2,1)}, u32[]{:S(2)}) copy-start(bf16[5,4,32,720]{3,2,1,0:T(8,128)(2,1)} %param.10) | copy-start | bytes 2764804
  5.9 1.0 %copy-start.4 = (s32[5,32,720]{2,1,0:T(8,128)S(1)}, s32[5,32,720]{2,1,0:T(8,128)}, u32[]{:S(2)}) copy-start(s32[5,32,720]{2,1,0:T(8,128)} %keep_ref.1) | copy-start | bytes 1382404
  6.9 0.8 %copy-start.5 = (f32[128,128]{1,0:T(8,128)S(1)}, f32[128,128]{1,0:T(8,128)}, u32[]{:S(2)}) copy-start(f32[128,128]{1,0:T(8,128)} %constant.5.clone.cosine_ref) | copy-start | bytes 196612
  7.8 0.7 %copy-start.6 = (f32[5,4,32]{2,1,0:T(4,128)S(1)}, f32[5,4,32]{2,1,0:T(4,128)}, u32[]{:S(2)}) copy-start(f32[5,4,32]{2,1,0:T(4,128)} %target_ref.1) | copy-start | bytes 7684
  8.5 0.7 %copy-start.7 = (f32[32]{0:T(128)S(1)}, f32[32]{0:T(128)}, u32[]{:S(2)}) copy-start(f32[32]{0:T(128)} %param.12) | copy-start | bytes 388

commit v3 on v2

--- a/solution.py
+++ b/solution.py
@@ -417,10 +417,10 @@
     mid_results = pl.pallas_call(
         functools.partial(kernel, sizes),
         out_shape=(
-            jax.ShapeDtypeStruct((bands, batch, levels), F32),
-            jax.ShapeDtypeStruct((pieces, 2, rows, columns), F32),
-            jax.ShapeDtypeStruct((pieces, 2, padded, columns), BF16),
-            jax.ShapeDtypeStruct((1, 1), F32),
+            pltpu.MemorySpace.VMEM((bands, batch, levels), F32),
+            pltpu.MemorySpace.VMEM((pieces, 2, rows, columns), F32),
+            pltpu.MemorySpace.VMEM((pieces, 2, padded, columns), BF16),
+            pltpu.MemorySpace.VMEM((1, 1), F32),
         ),
         in_specs=[in_hbm] * 5 + [inside] * 3,
         out_specs=(inside,) * 4,
@@ -449,7 +449,7 @@
             pltpu.SemaphoreType.DMA((groups,)),
         ],
         compiler_params=pltpu.CompilerParams(
-            collective_id=0, has_side_effects=True, vmem_limit_bytes=32 * 1024 * 1024
+            collective_id=0, has_side_effects=True, vmem_limit_bytes=56 * 1024 * 1024
         ),
     )(*fields, keep, table, cosine, depth.reshape(1, levels), target)
     psi, heat, moment, penalty = pl.pallas_call(

time: 62 us -> 54.1 us (0.87)
  local copies, waits for them, and re-layouts: 8.49 us -> 0 us
  Pallas kernels: 52.5 us -> 53.3 us
    unnamed x16 -> x0, local copies, waits for them, and re-layouts: 8.49 us -> none
    pallas_call x1, Pallas kernels: 49.9 us -> 50.8 us  [per_device(): pl.pallas_call(functools.partial(kernel, sizes), out_shape=(pltpu.MemoryS...]
where the time goes in v3:
time: 54.1 us; the launch traced here: 54 us
  Pallas kernels  53.3 us (99%)
  between operations  0.64 us (1%)
    pallas_call x1, Pallas kernels, per_device(): pl.pallas_call(functools.partial(kernel, sizes), out_shape=(pltpu.MemoryS...  50.8 us
    pallas_call x1, Pallas kernels, per_device(): pl.pallas_call(functools.partial(assemble, (bands, batch, levels, rows)),...  2.55 us

profile of v3, /device:TPU:0, one launch (start us, length us, event | category | flops | bytes accessed | tf_op | source)
XLA Modules:
  0.0 54.0 jit_solution(4829127902329547090)
XLA Ops:
  0.6 50.8 %shard_map.111 = (f32[5,4,32]{2,1,0:T(4,128)S(1)}, f32[3,2,360,128]{3,2,1,0:T(8,128)S(1)}, bf16[3,2,384,128]{3,2,1,0:T(8,128)(2,1)S(1)}, f32[1,1]{1,0:T(1,128)}) custom-call(bf16[5,128,720]{2,1,0:T(8,128)(2,1)} %bitcast.7, bf16[5,128,720]{2,1,0:T(8,128)(2,1)} %bitcast.8, bf16[5,128,720]{2,1,0:T(8,128)(2,1)} %bitcast.9, s32[5,32,720]{2,1,0:T(8,128)} %keep_ref.1, ...), custom_call_target="tpu_custom_call" | custom-call | tf_op jit(solution)/shard_map/pallas_call | solution.py:417
  51.4 2.6 %shard_map.112 = (f32[5,4,32]{2,1,0:T(4,128)}, f32[5,360,128]{2,1,0:T(8,128)}, f32[5,360,128]{2,1,0:T(8,128)}, f32[1,1]{1,0:T(1,128)}) custom-call(f32[5,4,32]{2,1,0:T(4,128)S(1)} %get-tuple-element.12.psi_in, f32[3,2,360,128]{3,2,1,0:T(8,128)S(1)} %get-tuple-element.13.own_ref, bf16[3,2,384,128]{3,2,1,0:T(8,128)(2,1)S(1)} %get-tuple-element.14.returned, ...), custom_call_target="tpu_custom_call" | custom-call | tf_op jit(solution)/shard_map/pallas_call | solution.py:455

commit v4 on v3

--- a/solution.py
+++ b/solution.py
@@ -84,19 +84,20 @@
     norm_factor = 2.0 / (4.0 * span * span)
     body = span // 128 * 128
     tail = span - body
-    whole = lambda step: (mine + step) % groups
+    strides = [2**bit for bit in range(groups.bit_length() - 1)]
+    across = lambda stride: mine + stride * (1 - 2 * ((mine // stride) % 2))
     place_of = lambda peer: {"lat": peer // lev_ways, "lev": peer % lev_ways}
 
     barrier = pltpu.get_barrier_semaphore()
     pl.semaphore_signal(barrier, inc=1, device_id=partner, device_id_type=pl.DeviceIdType.MESH)
 
-    def greet(step, carry):
+    for stride in strides:
         pl.semaphore_signal(
-            barrier, inc=1, device_id=place_of(whole(step)), device_id_type=pl.DeviceIdType.MESH
-        )
-        return carry
-
-    lax.fori_loop(1, groups, greet, 0)
+            barrier,
+            inc=1,
+            device_id=place_of(across(stride)),
+            device_id_type=pl.DeviceIdType.MESH,
+        )
 
     their_rows = [other * (half + mid) + i for i in range(half)]
     my_rows = [me * (half + mid) + i for i in range(half)]
@@ -156,7 +157,7 @@
     def send_row(piece, place):
         here = pack_row(piece, place)
         if place == 0:
-            pl.semaphore_wait(barrier, groups)
+            pl.semaphore_wait(barrier, 1 + len(strides))
         copy = remote(
             packed.at[piece, here, :],
             arrived.at[piece, here, :],
@@ -247,27 +248,25 @@
         own_ref[piece, 0] = heat[:rows]
         own_ref[piece, 1] = moment[:rows]
 
-    def mean_to(step):
-        peer = whole(step)
+    def mean_copy(step):
+        stride = strides[step]
+        block = pl.ds(mine // stride * stride, stride)
         return pltpu.make_async_remote_copy(
-            src_ref=mean_mine,
-            dst_ref=gathered.at[mine],
+            src_ref=gathered.at[block],
+            dst_ref=gathered.at[block],
             send_sem=mean_send.at[step],
-            recv_sem=mean_recv.at[mine],
-            device_id=place_of(peer),
+            recv_sem=mean_recv.at[step],
+            device_id=place_of(across(stride)),
             device_id_type=pl.DeviceIdType.MESH,
         )
 
-    def mean_from(step):
-        peer = whole(step)
-        return pltpu.make_async_remote_copy(
-            src_ref=mean_mine,
-            dst_ref=gathered.at[peer],
-            send_sem=mean_send.at[step],
-            recv_sem=mean_recv.at[peer],
-            device_id=place_of(peer),
-            device_id_type=pl.DeviceIdType.MESH,
-        )
+    mean_copies = [mean_copy(step) for step in range(len(strides))]
+
+    def pass_means(first, last):
+        for step in range(first, last):
+            if step > 0:
+                mean_copies[step - 1].wait_recv()
+            mean_copies[step].start()
 
     def share_means():
         zonal_copy.wait_recv()
@@ -278,18 +277,8 @@
         mean_mine[pl.ds(slab, bands), :] = target
         gathered[mine] = mean_mine[...]
 
-        def start(step, carry):
-            mean_to(step).start()
-            return carry
-
-        lax.fori_loop(1, groups, start, 0)
-
     def finish_stream():
-        def arrive(step, carry):
-            mean_from(step).wait_recv()
-            return carry
-
-        lax.fori_loop(1, groups, arrive, 0)
+        mean_copies[-1].wait_recv()
         height = groups * slab
         cosine = cosine_ref[...]
         depth = jnp.concatenate([depth_ref[...]] * batch, axis=1)
@@ -316,13 +305,18 @@
             psi_ref[:, b, :] = own[:, b * levels : (b + 1) * levels]
 
     pieces = mid + half
+    early_steps = max(len(strides) - 1, 1)
     for piece in range(pieces):
         if piece == min(1, pieces - 1):
             share_means()
-        if piece == pieces - 1:
-            finish_stream()
+            pass_means(0, 1)
         process(piece)
-
+        if piece == pieces - 2:
+            pass_means(1, early_steps)
+    if pieces < 2:
+        pass_means(1, early_steps)
+    pass_means(early_steps, len(strides))
+    finish_stream()
     for copies in back_copies:
         for copy in copies:
             copy.wait_recv()
@@ -331,11 +325,8 @@
             copy.wait_send()
     zonal_copy.wait_send()
 
-    def sent_all(step, carry):
-        mean_to(step).wait_send()
-        return carry
-
-    lax.fori_loop(1, groups, sent_all, 0)
+    for copy in mean_copies:
+        copy.wait_send()
 
 
 def assemble(sizes, psi_in, own_ref, returned, penalty_in, psi_ref, heat_ref, moment_ref, penalty_ref, stage, sems):
@@ -394,6 +385,7 @@
     assert lon_ways == 2
     lev_ways = mesh_shape["lev"]
     groups = mesh_shape["lat"] * lev_ways
+    assert groups > 1 and groups & (groups - 1) == 0
     rows = HARMONIC_ORDERS // lon_ways
     padded = round_up(rows, 128)
     rows_sent = round_up(rows, 16)

time: 54.1 us -> 51.6 us (0.954)
  Pallas kernels: 53.3 us -> 50.7 us
    pallas_call x1, Pallas kernels: 50.8 us -> 48.2 us  [per_device(): pl.pallas_call(functools.partial(kernel, sizes), out_shape=(pltpu.MemoryS...]
where the time goes in v4:
time: 51.6 us; the launch traced here: 51.4 us
  Pallas kernels  50.7 us (98%)
  between operations  0.64 us (1%)
    pallas_call x1, Pallas kernels, per_device(): pl.pallas_call(functools.partial(kernel, sizes), out_shape=(pltpu.MemoryS...  48.2 us
    pallas_call x1, Pallas kernels, per_device(): pl.pallas_call(functools.partial(assemble, (bands, batch, levels, rows)),...  2.55 us

profile of v4, /device:TPU:0, one launch (start us, length us, event | category | flops | bytes accessed | tf_op | source)
XLA Modules:
  0.0 51.4 jit_solution(3931958183002169418)
XLA Ops:
  0.6 48.2 %shard_map.111 = (f32[5,4,32]{2,1,0:T(4,128)S(1)}, f32[3,2,360,128]{3,2,1,0:T(8,128)S(1)}, bf16[3,2,384,128]{3,2,1,0:T(8,128)(2,1)S(1)}, f32[1,1]{1,0:T(1,128)}) custom-call(bf16[5,128,720]{2,1,0:T(8,128)(2,1)} %bitcast.7, bf16[5,128,720]{2,1,0:T(8,128)(2,1)} %bitcast.8, bf16[5,128,720]{2,1,0:T(8,128)(2,1)} %bitcast.9, s32[5,32,720]{2,1,0:T(8,128)} %keep_ref.1, ...), custom_call_target="tpu_custom_call" | custom-call | tf_op jit(solution)/shard_map/pallas_call | solution.py:409
  48.8 2.6 %shard_map.112 = (f32[5,4,32]{2,1,0:T(4,128)}, f32[5,360,128]{2,1,0:T(8,128)}, f32[5,360,128]{2,1,0:T(8,128)}, f32[1,1]{1,0:T(1,128)}) custom-call(f32[5,4,32]{2,1,0:T(4,128)S(1)} %get-tuple-element.12.psi_in, f32[3,2,360,128]{3,2,1,0:T(8,128)S(1)} %get-tuple-element.13.own_ref, bf16[3,2,384,128]{3,2,1,0:T(8,128)(2,1)S(1)} %get-tuple-element.14.returned, ...), custom_call_target="tpu_custom_call" | custom-call | tf_op jit(solution)/shard_map/pallas_call | solution.py:447
